TPU v7x, 256 devices: a whole 4x4x8 slice. The times are simulated.
256 devices in a mesh: seq: 64 (over z, y, core), head: 4 (over x).
Axes of the slice: x: 4, y: 4, z: 8, core: 2. Of those that a mesh axis runs over, the one named last changes fastest.
Arguments:
- tokens: bfloat16 [8192, 2048], P('seq'), may hold values from -20 to 20, as said below
- projection: bfloat16 [2048, 3072], P(None, 'head'), may hold values from -0.078125 to 0.078125
- context_cotangent: bfloat16 [8192, 2048], P('seq', 'head'), may hold values from -80 to 80
Outputs:
- perturbed_context: bfloat16 [8192, 2048], P('seq', 'head')
- ascent_direction: float32 [2048, 3072], P('seq', 'head')
Inputs may be any that keep to these rules, and one draw needn't show every extreme that they name: `tokens`: activations of the layer.
All inputs are finite; a program needn't handle non-finite values.
Results may differ from a plain program's by a relative error of at most 0.017.
Values may be sent and summed in bfloat16 or wider, within the bound.
No kernel may reach another device: no remote copies, remote signals or barrier semaphores. Data moves between devices by JAX's collectives and lax.ppermute only.
A program may use at most 64 MiB of HBM per device.

v0:
```python
import math
import jax
import jax.numpy as jnp
from jax import lax
from jax.sharding import Mesh
from jax.sharding import PartitionSpec as P

INPUT_FEATURES = 2048
KEY_VALUE_HEADS = 4
HEAD_DIMENSION = 128
QUERY_PER_GROUP = 4
SEQ = ("seq_0", "seq_1", "seq_2")
masked_score = -1e30
key_block = 512


def scatter_axes(shard, axes, dim):
    for axis in axes:
        shard = lax.psum_scatter(shard, axis, scatter_dimension=dim, tiled=True)
    return shard


def sent_to_all(shard, axis):
    length = lax.axis_size(axis)
    return lax.all_to_all(
        jnp.broadcast_to(shard[None], (length, *shard.shape)), axis, 0, 0, tiled=True
    )


def taken_together(shard, axis):
    everything = sent_to_all(shard, axis)
    return jnp.sum(everything, axis=0)


def joined_along(tiles, dim):
    tiles = jnp.moveaxis(tiles, 0, dim)
    dims = tiles.shape
    return tiles.reshape(*dims[:dim], dims[dim] * dims[dim + 1], *dims[dim + 2 :])


def stacked_from(shard, axes, turns):
    tiles = shard[None]
    for k in turns:
        tiles = lax.all_gather(tiles, axes[k], axis=0, tiled=True)
    carried = [lax.axis_size(axes[k]) for k in reversed(turns)]
    tiles = tiles.reshape(*carried, *shard.shape)
    turned = sorted(range(len(turns)), key=lambda place: turns[len(turns) - 1 - place])
    return tiles.transpose(*turned, *range(len(turns), tiles.ndim)).reshape(-1, *shard.shape)


def gathered_by_axis(shard, axes, turns, dim):
    return joined_along(stacked_from(shard, axes, turns), dim)


def attend_fold(query_rows, query_pos, score_scale):
    head_size = query_rows.shape[1]

    def single_block(carry_state, block_rows, offset):
        running_max, row_total, context_sum = carry_state
        key_rows = block_rows[:, :head_size]
        value_rows = block_rows[:, head_size:].astype(jnp.float32)
        scores = jnp.dot(query_rows, key_rows.T, preferred_element_type=jnp.float32) * score_scale
        key_pos = offset + jnp.arange(block_rows.shape[0], dtype=jnp.int32)
        allowed = key_pos[None, :] <= query_pos[:, None]
        scores = jnp.where(allowed, scores, masked_score)
        new_max = jnp.maximum(running_max, jnp.max(scores, axis=1))
        factor = jnp.exp(running_max - new_max)
        weights = jnp.where(allowed, jnp.exp(scores - new_max[:, None]), 0.0)
        row_total = row_total * factor + jnp.sum(weights, axis=1)
        context_sum = context_sum * factor[:, None] + jnp.dot(
            weights, value_rows, preferred_element_type=jnp.float32
        )
        return (new_max, row_total, context_sum)

    def fold_keys(carry_state, block_rows, offset):
        row_count = block_rows.shape[0]
        if row_count > key_block and row_count % key_block == 0:

            def sub_block(block_index, inner_state):
                part_rows = lax.dynamic_slice_in_dim(
                    block_rows, block_index * key_block, key_block, 0
                )
                return single_block(inner_state, part_rows, block_index * key_block)

            return lax.fori_loop(0, row_count // key_block, sub_block, carry_state)
        return single_block(carry_state, block_rows, offset)

    return fold_keys


def on_device(tokens, projection, context_cotangent):
    score_scale = HEAD_DIMENSION ** (-0.5)
    local_rows = tokens.shape[0]
    rows_all = local_rows * QUERY_PER_GROUP
    first_row = lax.axis_index(SEQ) * local_rows
    query_pos = first_row + jnp.arange(rows_all, dtype=jnp.int32) // QUERY_PER_GROUP

    def split_heads(projected_weight):
        reshaped_grads = projected_weight.reshape(local_rows, QUERY_PER_GROUP + 2, HEAD_DIMENSION)
        query_rows = reshaped_grads[:, :QUERY_PER_GROUP].reshape(rows_all, HEAD_DIMENSION)
        key_value = reshaped_grads[:, QUERY_PER_GROUP:].reshape(local_rows, 2 * HEAD_DIMENSION)
        return (query_rows, key_value)

    def empty_state():
        return (
            jnp.full((rows_all,), masked_score, jnp.float32),
            jnp.zeros((rows_all,), jnp.float32),
            jnp.zeros((rows_all, HEAD_DIMENSION), jnp.float32),
        )

    projected_weight = jnp.dot(tokens, projection, preferred_element_type=jnp.float32).astype(
        jnp.bfloat16
    )
    query_rows, key_value = split_heads(projected_weight)
    gathered = lax.all_gather(key_value, SEQ, axis=0, tiled=True)
    total_rows = gathered.shape[0]
    block_size = min(key_block, total_rows)
    needed = (first_row + local_rows - 1) // block_size + 1
    fold_first = attend_fold(query_rows, query_pos, score_scale)

    def forward_step(block_index, carry_state):
        block_rows = lax.dynamic_slice_in_dim(gathered, block_index * block_size, block_size, 0)
        return fold_first(carry_state, block_rows, block_index * block_size)

    running_max, row_total, context_sum = lax.fori_loop(0, needed, forward_step, empty_state())
    context = (context_sum / row_total[:, None]).astype(jnp.bfloat16)
    log_total = running_max + jnp.log(row_total)
    grad_rows = context_cotangent.reshape(rows_all, HEAD_DIMENSION)
    row_delta = jnp.sum(grad_rows.astype(jnp.float32) * context.astype(jnp.float32), axis=1)
    contract_rows = (((0,), (0,)), ((), ()))

    def backward_step(block_index, carry_state):
        query_grad, key_terms = carry_state
        offset = block_index * block_size
        block_rows = lax.dynamic_slice_in_dim(gathered, offset, block_size, 0)
        key_rows = block_rows[:, :HEAD_DIMENSION]
        value_rows = block_rows[:, HEAD_DIMENSION:]
        scores = jnp.dot(query_rows, key_rows.T, preferred_element_type=jnp.float32) * score_scale
        key_pos = offset + jnp.arange(block_size, dtype=jnp.int32)
        allowed = key_pos[None, :] <= query_pos[:, None]
        probs_full = jnp.where(allowed, jnp.exp(scores - log_total[:, None]), 0.0)
        probs_half = probs_full.astype(jnp.bfloat16)
        prob_grad = jnp.dot(grad_rows, value_rows.T, preferred_element_type=jnp.float32)
        score_grad = (probs_full * (prob_grad - row_delta[:, None]) * score_scale).astype(
            jnp.bfloat16
        )
        query_grad = query_grad + jnp.dot(score_grad, key_rows, preferred_element_type=jnp.float32)
        key_grad = lax.dot_general(
            score_grad, query_rows, contract_rows, preferred_element_type=jnp.float32
        )
        value_grad = lax.dot_general(
            probs_half, grad_rows, contract_rows, preferred_element_type=jnp.float32
        )
        key_terms = lax.dynamic_update_slice_in_dim(
            key_terms, jnp.concatenate([key_grad, value_grad], axis=1), offset, 0
        )
        return (query_grad, key_terms)

    initial = (
        jnp.zeros((rows_all, HEAD_DIMENSION), jnp.float32),
        jnp.zeros((total_rows, 2 * HEAD_DIMENSION), jnp.float32),
    )
    query_grad, key_terms = lax.fori_loop(0, needed, backward_step, initial)
    key_value_grad = scatter_axes(key_terms, SEQ, 0).astype(jnp.bfloat16)
    head_grads = jnp.concatenate(
        [
            query_grad.astype(jnp.bfloat16).reshape(local_rows, QUERY_PER_GROUP * HEAD_DIMENSION),
            key_value_grad,
        ],
        axis=1,
    )
    grad_term = lax.dot_general(
        tokens, head_grads, contract_rows, preferred_element_type=jnp.float32
    )
    normalizing_scale = math.sqrt(
        INPUT_FEATURES * KEY_VALUE_HEADS * (QUERY_PER_GROUP + 2) * HEAD_DIMENSION
    )
    ascent_radius = 0.2 * math.sqrt(KEY_VALUE_HEADS * (QUERY_PER_GROUP + 2) * HEAD_DIMENSION)
    weight_grad = lax.psum(grad_term, SEQ)
    square_sum = taken_together(jnp.sum(weight_grad * weight_grad), "head")
    grad_norm = jnp.sqrt(square_sum)
    share_rows = INPUT_FEATURES // lax.axis_size(SEQ)
    own_grad = lax.dynamic_slice_in_dim(
        weight_grad, lax.axis_index(SEQ) * share_rows, share_rows, 0
    )
    direction = own_grad * (normalizing_scale / grad_norm)
    moved_weights = (
        projection.astype(jnp.float32) + ascent_radius / grad_norm * weight_grad
    ).astype(jnp.bfloat16)
    projected_new = jnp.dot(tokens, moved_weights, preferred_element_type=jnp.float32).astype(
        jnp.bfloat16
    )
    query_new, key_value_new = split_heads(projected_new)
    fold_new = attend_fold(query_new, query_pos, score_scale)
    final_state = fold_new(
        empty_state(), gathered_by_axis(key_value_new, SEQ, (1, 0, 2), 0), jnp.int32(0)
    )
    perturbed = (
        (final_state[2] / final_state[1][:, None])
        .astype(jnp.bfloat16)
        .reshape(local_rows, QUERY_PER_GROUP * HEAD_DIMENSION)
    )
    return (perturbed, direction)


def solution(mesh):
    finer = Mesh(
        mesh.devices.reshape(8, 4, 2, mesh.shape["head"]), ("seq_0", "seq_1", "seq_2", "head")
    )
    placed = (P(SEQ, None), P(None, "head"), P(SEQ, "head"))
    return jax.shard_map(
        on_device,
        mesh=finer,
        in_specs=placed,
        out_specs=(P(SEQ, "head"), P(SEQ, "head")),
        check_vma=False,
    )
```

profile of v0, /device:TPU:1, one launch (start us, length us, event | category | flops | bytes accessed | tf_op | source)
XLA Modules:
  0.0 723.9 jit_solution(13365416468607866390)
XLA Ops:
  7.2 1.0 copy-done
  8.2 2.5 convolution_convert_fusion
  10.9 0.7 copy.51
  12.0 83.2 %all-gather.4.cloned.1.call-done = bf16[8192,256]{1,0:T(8,128)(2,1)} async-done(((bf16[128,256]{1,0:T(8,128)(2,1)}), bf16[8192,256]{1,0:T(8,128)(2,1)}) %all-gather.4.cloned.1.call-update) | async-done | bytes 4194320 | tf_op jit(solution)/shard_map/all_gather | solution.py:115
  95.2 3.0 while.46
  95.3 1.2 fusion.107
  96.8 1.4 convolution_add_fusion.6
  98.5 4.2 broadcast_in_dim.56
  102.7 5.3 while.47
  102.7 1.3 fusion.120
  104.0 1.2 fusion.121
  105.2 1.3 convolution_add_fusion.7
  107.1 0.9 maximum_dynamic-update-slice_fusion.2
  108.1 214.4 %reduce-scatter.4.cloned.1.call-done = f32[1024,256]{0,1:T(8,128)} async-done(((f32[8192,256]{0,1:T(8,128)}), f32[1024,256]{0,1:T(8,128)}) %reduce-scatter.4.cloned.1.call-update) | async-done | bytes 1048592 | tf_op jit(solution)/shard_map/reduce_scatter | solution.py:19
  322.6 26.0 %reduce-scatter.6.cloned.1.call-done = f32[256,256]{0,1:T(8,128)} async-done(((f32[1024,256]{0,1:T(8,128)}), f32[256,256]{0,1:T(8,128)}) %reduce-scatter.6.cloned.1.call-update) | async-done | bytes 262160 | tf_op jit(solution)/shard_map/reduce_scatter | solution.py:19
  348.8 17.3 %reduce-scatter.8.cloned.1.call-done = f32[128,256]{0,1:T(8,128)} async-done(((f32[256,256]{0,1:T(8,128)}), f32[128,256]{0,1:T(8,128)}) %reduce-scatter.8.cloned.1.call-update) | async-done | bytes 131088 | tf_op jit(solution)/shard_map/reduce_scatter | solution.py:19
  366.1 0.9 convert_element_type.49
  367.1 3.7 convolution_bitcast_fusion
  370.8 4.7 copy.49
  375.5 195.1 %all-reduce.2.cloned.1.call-done = f32[2048,768]{0,1:T(8,128)} async-done(((f32[2048,768]{0,1:T(8,128)}), f32[2048,768]{0,1:T(8,128)}) %all-reduce.2.cloned.1.call-update) | async-done | bytes 6291472 | tf_op jit(solution)/shard_map/psum | solution.py:179
  570.6 5.0 multiply_reduce_fusion
  575.6 0.6 broadcast_in_dim.57
  576.3 7.9 %all_to_all.6 = f32[4,1,1]{2,1,0:T(1,128)S(1)} all-to-all(f32[4,1,1]{2,1,0:T(1,128)S(1)} %broadcast_in_dim.57), channel_id=1, replica_groups=mesh['seq_0'=8,'seq_1'=4,'seq_2'=2,'head'=4] {'head'}, dimensions={0} | all-to-all | bytes 32 | tf_op jit(solution)/shard_map/all_to_all | solution.py:25
  585.5 4.7 fusion.58
  590.4 10.1 %all_gather.13 = bf16[4,128,256]{2,1,0:T(8,128)(2,1)} all-gather(bf16[1,128,256]{2,1,0:T(8,128)(2,1)S(1)} %copy.59), channel_id=1, replica_groups=mesh['seq_0'=8,'seq_1'=4,'seq_2'=2,'head'=4] {'seq_1'}, dimensions={0}, use_global_device_ids=true | all-gather | bytes 327680 | tf_op jit(solution)/shard_map/all_gather | solution.py:44
  600.6 39.3 %all-gather.6.cloned.1.call-done = bf16[32,128,256]{2,1,0:T(8,128)(2,1)} async-done(((bf16[4,128,256]{2,1,0:T(8,128)(2,1)}), bf16[32,128,256]{2,1,0:T(8,128)(2,1)}) %all-gather.6.cloned.1.call-update) | async-done | bytes 2097168 | tf_op jit(solution)/shard_map/all_gather | solution.py:44
  640.1 1.2 dynamic-slice_multiply_fusion
  641.3 0.8 copy.58
  642.1 22.1 %all-gather.8.cloned.1.call-done = bf16[64,128,256]{2,1,0:T(8,128)(2,1)} async-done(((bf16[32,128,256]{2,1,0:T(8,128)(2,1)}), bf16[64,128,256]{2,1,0:T(8,128)(2,1)}) %all-gather.8.cloned.1.call-update) | async-done | bytes 4194320 | tf_op jit(solution)/shard_map/all_gather | solution.py:44
  664.2 4.6 copy.56
  668.8 47.4 %while.48 = (s32[]{:T(128)}, f32[512]{0:T(512)S(1)}, f32[512]{0:T(512)S(1)}, f32[512,128]{1,0:T(8,128)S(1)}, bf16[8192,256]{1,0:T(8,128)(2,1)}, /*index=5*/bf16[...) while((s32[]{:T(128)}, f32[512]{0:T(512)S(1)}, ...), condition=%wide.region_16.17_spmd.clone, body=%wide.region_13.16_spmd.clone.sunk | while | flops 137305600 | bytes 4112599 | solution.py:85
  668.8 1.2 fusion.127
  670.3 1.4 convolution_add_fusion.8
  671.7 1.2 fusion.127
  673.3 1.4 convolution_add_fusion.8
  674.7 1.2 fusion.127
  676.2 1.4 convolution_add_fusion.8
  677.7 1.2 fusion.127
  679.2 1.4 convolution_add_fusion.8
  680.6 1.2 fusion.127
  682.2 1.4 convolution_add_fusion.8
  683.6 1.2 fusion.127
  685.1 1.4 convolution_add_fusion.8
  686.6 1.2 fusion.127
  688.1 1.4 convolution_add_fusion.8
  689.5 1.2 fusion.127
  691.0 1.4 convolution_add_fusion.8
  692.5 1.2 fusion.127
  694.0 1.4 convolution_add_fusion.8
  695.5 1.2 fusion.127
  697.0 1.4 convolution_add_fusion.8
  698.4 1.2 fusion.127
  699.9 1.4 convolution_add_fusion.8
  701.4 1.2 fusion.127
  702.9 1.4 convolution_add_fusion.8
  704.4 1.2 fusion.127
  705.9 1.4 convolution_add_fusion.8
  707.3 1.2 fusion.127
  708.8 1.4 convolution_add_fusion.8
  710.3 1.2 fusion.127
  711.8 1.4 convolution_add_fusion.8
  713.2 1.2 fusion.127
  714.8 1.4 convolution_add_fusion.8
  716.3 0.7 reshape.65
  (128 shorter events, 7.5 us)
Async XLA Ops:
  7.2 1.0 copy-start
  7.2 4.7 copy-start.1
  7.2 88.0 %all-gather.4.cloned.1.call-start = ((), (), s32[]{:S(2)}) async-start(), calls=%async_computation.4 | async-start | bytes 4259840 | tf_op jit(solution)/shard_map/all_gather | solution.py:115
  11.6 310.9 %reduce-scatter.4.cloned.1.call-start = ((), (), s32[]{:S(2)}) async-start(), calls=%async_computation.5 | async-start | bytes 9437184 | tf_op jit(solution)/shard_map/reduce_scatter | solution.py:19
  108.0 240.5 %reduce-scatter.6.cloned.1.call-start = ((), (), s32[]{:S(2)}) async-start(), calls=%async_computation.6 | async-start | bytes 1310720 | tf_op jit(solution)/shard_map/reduce_scatter | solution.py:19
  322.5 43.5 %reduce-scatter.8.cloned.1.call-start = ((), (), s32[]{:S(2)}) async-start(), calls=%async_computation.7 | async-start | bytes 393216 | tf_op jit(solution)/shard_map/reduce_scatter | solution.py:19
  348.6 222.0 %all-reduce.2.cloned.1.call-start = ((), (), s32[]{:S(2)}) async-start(), calls=%async_computation.8 | async-start | bytes 12582912 | tf_op jit(solution)/shard_map/psum | solution.py:179
  370.8 269.1 %all-gather.6.cloned.1.call-start = ((), (), s32[]{:S(2)}) async-start(), calls=%async_computation.9 | async-start | bytes 2359296 | tf_op jit(solution)/shard_map/all_gather | solution.py:44
  600.5 63.6 %all-gather.8.cloned.1.call-start = ((), (), s32[]{:S(2)}) async-start(), calls=%async_computation.10 | async-start | bytes 6291456 | tf_op jit(solution)/shard_map/all_gather | solution.py:44
Sparse Core Ops, SparseCore 0:
  11.8 83.3 all-gather.3
  108.2 214.2 reduce-scatter.3
  325.0 23.4 reduce-scatter.5
  350.9 15.0 reduce-scatter.7
  370.9 199.6 all-reduce.1
  600.6 39.1 all-gather.5
  641.7 22.4 all-gather.7
where the time goes:
time: 726 us; the launch traced here: 724 us
  waiting for transfers between devices  598 us (82%)
  matrix products  60.1 us (8%)
  local copies, waits for them, and re-layouts  18.4 us (3%)
  blocking collectives  18 us (2%)
  between operations  15.1 us (2%)
  other arithmetic  13.5 us (2%)
    reduce_scatter x3, waiting for transfers between devices, scatter_axes(): shard = lax.psum_scatter(shard, axis, scatter_dimension=dim, tiled=True)  258 us
    psum x1, waiting for transfers between devices, on_device(): weight_grad = lax.psum(grad_term, SEQ)  195 us
    all_gather x1, waiting for transfers between devices, on_device(): gathered = lax.all_gather(key_value, SEQ, axis=0, tiled=True)  83.2 us
    all_gather x2, waiting for transfers between devices, stacked_from(): tiles = lax.all_gather(tiles, axes[k], axis=0, tiled=True)  61.4 us
    dot_general x17, matrix products, single_block(): jnp.dot(weights, value_rows, preferred_element_type=jnp.float32)  23.9 us
    dot_general x17, matrix products, single_block(): jnp.dot(query_rows, key_rows.T, preferred_element_type=jnp.float32)  20.9 us
  transfers between devices with their start and end apart: 7, of which 7 were waited for; matrix products, arithmetic and copies ran while one was open for 1% of the time, Pallas kernels for 0%

commit v1 on v0

--- a/solution.py
+++ b/solution.py
@@ -176,7 +176,7 @@
         INPUT_FEATURES * KEY_VALUE_HEADS * (QUERY_PER_GROUP + 2) * HEAD_DIMENSION
     )
     ascent_radius = 0.2 * math.sqrt(KEY_VALUE_HEADS * (QUERY_PER_GROUP + 2) * HEAD_DIMENSION)
-    weight_grad = lax.psum(grad_term, SEQ)
+    weight_grad = lax.psum(lax.psum(grad_term, "seq_0"), ("seq_1", "seq_2"))
     square_sum = taken_together(jnp.sum(weight_grad * weight_grad), "head")
     grad_norm = jnp.sqrt(square_sum)
     share_rows = INPUT_FEATURES // lax.axis_size(SEQ)

time: 726 us -> 766 us (1.055)
  waiting for transfers between devices: 598 us -> 636 us
    psum x1 -> x2, waiting for transfers between devices: 195 us -> 234 us  [on_device(): weight_grad = lax.psum(lax.psum(grad_term, 'seq_0'), ('seq_1', 'seq_2'))]
  transfers between devices with their start and end apart: 7 -> 8, of which waited for: 7 -> 8; matrix products, arithmetic and copies ran while one was open for 1% -> 1% of each run, Pallas kernels for 0% -> 0%
where the time goes in v1:
time: 766 us; the launch traced here: 763 us
  waiting for transfers between devices  636 us (83%)
  matrix products  60 us (8%)
  local copies, waits for them, and re-layouts  18.4 us (2%)
  blocking collectives  18.4 us (2%)
  between operations  15.1 us (2%)
  other arithmetic  13.5 us (2%)
    reduce_scatter x3, waiting for transfers between devices, scatter_axes(): shard = lax.psum_scatter(shard, axis, scatter_dimension=dim, tiled=True)  258 us
    psum x2, waiting for transfers between devices, on_device(): weight_grad = lax.psum(lax.psum(grad_term, 'seq_0'), ('seq_1', 'seq_2'))  234 us
    all_gather x1, waiting for transfers between devices, on_device(): gathered = lax.all_gather(key_value, SEQ, axis=0, tiled=True)  83.2 us
    all_gather x2, waiting for transfers between devices, stacked_from(): tiles = lax.all_gather(tiles, axes[k], axis=0, tiled=True)  61.1 us
    dot_general x17, matrix products, single_block(): jnp.dot(weights, value_rows, preferred_element_type=jnp.float32)  23.9 us
    dot_general x17, matrix products, single_block(): jnp.dot(query_rows, key_rows.T, preferred_element_type=jnp.float32)  20.9 us
  transfers between devices with their start and end apart: 8, of which 8 were waited for; matrix products, arithmetic and copies ran while one was open for 1% of the time, Pallas kernels for 0%

profile of v1, /device:TPU:1, one launch (start us, length us, event | category | flops | bytes accessed | tf_op | source)
XLA Modules:
  0.0 763.3 jit_solution(11717293769317625916)
XLA Ops:
  7.2 1.0 copy-done
  8.2 2.5 convolution_convert_fusion
  10.9 0.7 copy.51
  12.0 83.2 %all-gather.4.cloned.1.call-done = bf16[8192,256]{1,0:T(8,128)(2,1)} async-done(((bf16[128,256]{1,0:T(8,128)(2,1)}), bf16[8192,256]{1,0:T(8,128)(2,1)}) %all-gather.4.cloned.1.call-update) | async-done | bytes 4194320 | tf_op jit(solution)/shard_map/all_gather | solution.py:115
  95.2 3.0 while.46
  95.3 1.2 fusion.107
  96.8 1.4 convolution_add_fusion.6
  98.5 4.2 broadcast_in_dim.56
  102.7 5.3 while.47
  102.7 1.3 fusion.120
  104.0 1.2 fusion.121
  105.2 1.3 convolution_add_fusion.7
  107.1 0.9 maximum_dynamic-update-slice_fusion.2
  108.1 214.4 %reduce-scatter.4.cloned.1.call-done = f32[1024,256]{0,1:T(8,128)} async-done(((f32[8192,256]{0,1:T(8,128)}), f32[1024,256]{0,1:T(8,128)}) %reduce-scatter.4.cloned.1.call-update) | async-done | bytes 1048592 | tf_op jit(solution)/shard_map/reduce_scatter | solution.py:19
  322.6 26.0 %reduce-scatter.6.cloned.1.call-done = f32[256,256]{0,1:T(8,128)} async-done(((f32[1024,256]{0,1:T(8,128)}), f32[256,256]{0,1:T(8,128)}) %reduce-scatter.6.cloned.1.call-update) | async-done | bytes 262160 | tf_op jit(solution)/shard_map/reduce_scatter | solution.py:19
  348.8 17.3 %reduce-scatter.8.cloned.1.call-done = f32[128,256]{0,1:T(8,128)} async-done(((f32[256,256]{0,1:T(8,128)}), f32[128,256]{0,1:T(8,128)}) %reduce-scatter.8.cloned.1.call-update) | async-done | bytes 131088 | tf_op jit(solution)/shard_map/reduce_scatter | solution.py:19
  366.1 0.9 convert_element_type.49
  367.1 3.7 convolution_bitcast_fusion
  370.8 148.9 %all-reduce.3.cloned.1.call-done = f32[2048,768]{0,1:T(8,128)} async-done(((f32[2048,768]{0,1:T(8,128)}), f32[2048,768]{0,1:T(8,128)}) %all-reduce.3.cloned.1.call-update) | async-done | bytes 6291472 | tf_op jit(solution)/shard_map/psum | solution.py:179
  519.8 4.7 copy.49
  524.5 85.4 %all-reduce.5.cloned.1.call-done = f32[2048,768]{0,1:T(8,128)} async-done(((f32[2048,768]{0,1:T(8,128)}), f32[2048,768]{0,1:T(8,128)}) %all-reduce.5.cloned.1.call-update) | async-done | bytes 6291472 | tf_op jit(solution)/shard_map/psum | solution.py:179
  609.9 5.0 multiply_reduce_fusion
  615.5 7.9 %all_to_all.6 = f32[4,1,1]{2,1,0:T(1,128)S(1)} all-to-all(f32[4,1,1]{2,1,0:T(1,128)S(1)} %broadcast_in_dim.57), channel_id=1, replica_groups=mesh['seq_0'=8,'seq_1'=4,'seq_2'=2,'head'=4] {'head'}, dimensions={0} | all-to-all | bytes 32 | tf_op jit(solution)/shard_map/all_to_all | solution.py:25
  624.8 4.7 fusion.58
  629.6 10.4 %all_gather.13 = bf16[4,128,256]{2,1,0:T(8,128)(2,1)} all-gather(bf16[1,128,256]{2,1,0:T(8,128)(2,1)S(1)} %copy.59), channel_id=1, replica_groups=mesh['seq_0'=8,'seq_1'=4,'seq_2'=2,'head'=4] {'seq_1'}, dimensions={0}, use_global_device_ids=true | all-gather | bytes 327680 | tf_op jit(solution)/shard_map/all_gather | solution.py:44
  640.1 39.1 %all-gather.6.cloned.1.call-done = bf16[32,128,256]{2,1,0:T(8,128)(2,1)} async-done(((bf16[4,128,256]{2,1,0:T(8,128)(2,1)}), bf16[32,128,256]{2,1,0:T(8,128)(2,1)}) %all-gather.6.cloned.1.call-update) | async-done | bytes 2097168 | tf_op jit(solution)/shard_map/all_gather | solution.py:44
  679.5 1.2 dynamic-slice_multiply_fusion
  680.7 0.8 copy.58
  681.4 22.1 %all-gather.8.cloned.1.call-done = bf16[64,128,256]{2,1,0:T(8,128)(2,1)} async-done(((bf16[32,128,256]{2,1,0:T(8,128)(2,1)}), bf16[64,128,256]{2,1,0:T(8,128)(2,1)}) %all-gather.8.cloned.1.call-update) | async-done | bytes 4194320 | tf_op jit(solution)/shard_map/all_gather | solution.py:44
  703.5 4.6 copy.56
  708.1 47.4 %while.48 = (s32[]{:T(128)}, f32[512]{0:T(512)S(1)}, f32[512]{0:T(512)S(1)}, f32[512,128]{1,0:T(8,128)S(1)}, bf16[8192,256]{1,0:T(8,128)(2,1)}, /*index=5*/bf16[...) while((s32[]{:T(128)}, f32[512]{0:T(512)S(1)}, ...), condition=%wide.region_17.18_spmd.clone, body=%wide.region_14.17_spmd.clone.sunk | while | flops 137305600 | bytes 4112599 | solution.py:85
  708.1 1.2 fusion.127
  709.7 1.4 convolution_add_fusion.8
  711.1 1.2 fusion.127
  712.6 1.4 convolution_add_fusion.8
  714.1 1.2 fusion.127
  715.6 1.4 convolution_add_fusion.8
  717.0 1.2 fusion.127
  718.5 1.4 convolution_add_fusion.8
  720.0 1.2 fusion.127
  721.5 1.4 convolution_add_fusion.8
  723.0 1.2 fusion.127
  724.5 1.4 convolution_add_fusion.8
  725.9 1.2 fusion.127
  727.4 1.4 convolution_add_fusion.8
  728.9 1.2 fusion.127
  730.4 1.4 convolution_add_fusion.8
  731.8 1.2 fusion.127
  733.4 1.4 convolution_add_fusion.8
  734.8 1.2 fusion.127
  736.3 1.4 convolution_add_fusion.8
  737.8 1.2 fusion.127
  739.3 1.4 convolution_add_fusion.8
  740.7 1.2 fusion.127
  742.3 1.4 convolution_add_fusion.8
  743.7 1.2 fusion.127
  745.2 1.4 convolution_add_fusion.8
  746.7 1.2 fusion.127
  748.2 1.4 convolution_add_fusion.8
  749.6 1.2 fusion.127
  751.1 1.4 convolution_add_fusion.8
  752.6 1.2 fusion.127
  754.1 1.4 convolution_add_fusion.8
  755.7 0.7 reshape.65
  (131 shorter events, 8.2 us)
Async XLA Ops:
  7.2 1.0 copy-start
  7.2 4.7 copy-start.1
  7.2 88.0 %all-gather.4.cloned.1.call-start = ((), (), s32[]{:S(2)}) async-start(), calls=%async_computation.4 | async-start | bytes 4259840 | tf_op jit(solution)/shard_map/all_gather | solution.py:115
  11.6 310.9 %reduce-scatter.4.cloned.1.call-start = ((), (), s32[]{:S(2)}) async-start(), calls=%async_computation.5 | async-start | bytes 9437184 | tf_op jit(solution)/shard_map/reduce_scatter | solution.py:19
  108.0 240.5 %reduce-scatter.6.cloned.1.call-start = ((), (), s32[]{:S(2)}) async-start(), calls=%async_computation.6 | async-start | bytes 1310720 | tf_op jit(solution)/shard_map/reduce_scatter | solution.py:19
  322.5 43.5 %reduce-scatter.8.cloned.1.call-start = ((), (), s32[]{:S(2)}) async-start(), calls=%async_computation.7 | async-start | bytes 393216 | tf_op jit(solution)/shard_map/reduce_scatter | solution.py:19
  348.6 171.1 %all-reduce.3.cloned.1.call-start = ((), (), s32[]{:S(2)}) async-start(), calls=%async_computation.8 | async-start | bytes 12582912 | tf_op jit(solution)/shard_map/psum | solution.py:179
  370.8 239.1 %all-reduce.5.cloned.1.call-start = ((), (), s32[]{:S(2)}) async-start(), calls=%async_computation.9 | async-start | bytes 12582912 | tf_op jit(solution)/shard_map/psum | solution.py:179
  519.8 159.5 %all-gather.6.cloned.1.call-start = ((), (), s32[]{:S(2)}) async-start(), calls=%async_computation.10 | async-start | bytes 2359296 | tf_op jit(solution)/shard_map/all_gather | solution.py:44
  640.1 63.4 %all-gather.8.cloned.1.call-start = ((), (), s32[]{:S(2)}) async-start(), calls=%async_computation.11 | async-start | bytes 6291456 | tf_op jit(solution)/shard_map/all_gather | solution.py:44
Sparse Core Ops, SparseCore 0:
  11.8 83.3 all-gather.3
  108.2 214.2 reduce-scatter.3
  325.0 23.4 reduce-scatter.5
  350.9 15.0 reduce-scatter.7
  370.9 148.8 all-reduce.2
  522.0 87.8 all-reduce.4
  640.2 38.9 all-gather.5
  681.0 22.4 all-gather.7
